TPU v7x, 32 devices: a whole 2x2x4 slice. The times are simulated.
32 devices in a mesh: cluster: 4 (over y, x), member: 8 (over z, core).
Axes of the slice: x: 2, y: 2, z: 4, core: 2. Of those that a mesh axis runs over, the one named last changes fastest.
Arguments:
- embeddings: bfloat16 [8192, 4096], P(('cluster', 'member')), may hold values from -15 to 15, as said below
- start_basis: bfloat16 [4096, 512], P(('cluster', 'member')), may hold values from -6 to 6
- cluster_ids: int32 [8192], P(('cluster', 'member')), may hold values from 0 to 7
- valid_counts: int32 [4], P('cluster'), may hold values from 512 to 2048
Outputs:
- subspace: float32 [4096, 512], P(('cluster', 'member'))
- nearest: float32 [8192], P(('cluster', 'member'))
Inputs may be any that keep to these rules, and one draw needn't show every extreme that they name: `embeddings`: Real-valued entries.
All inputs are finite; a program needn't handle non-finite values.
Results may differ from a plain program's by a relative error of at most 0.0042.
Values may be sent and summed in bfloat16 or wider, within the bound.
No kernel may reach another device: no remote copies, remote signals or barrier semaphores. Data moves between devices by JAX's collectives and lax.ppermute only.
A program may use at most 64 MiB of HBM per device.

v0:
```python
import math
import jax
import jax.numpy as jnp
from jax import lax
from jax.sharding import PartitionSpec as P

D = 4096
ITERS = 2
EPS = 1e-06


def spread_basis(local_rows):
    return lax.all_gather(local_rows, ("cluster", "member"), axis=0, tiled=True)


def reduce_image(centered, projected):
    return lax.psum_scatter(
        lax.dot_general(
            centered, projected, (((0,), (0,)), ((), ())), preferred_element_type=jnp.float32
        ),
        ("cluster", "member"),
        scatter_dimension=0,
        tiled=True,
    )


def body(embeddings, start_basis, cluster_ids, valid_counts):
    row_count = embeddings.shape[0]
    total_rows = row_count * lax.axis_size(("cluster", "member"))
    ones_row = jnp.ones((1, row_count), jnp.bfloat16)
    column_sums = jnp.dot(ones_row, embeddings, preferred_element_type=jnp.float32)[0]
    average = lax.psum(column_sums, ("cluster", "member")) / total_rows
    centered = (embeddings.astype(jnp.float32) - average).astype(jnp.bfloat16)
    basis_full = spread_basis(start_basis)
    orthonormal = None
    for sweep in range(ITERS):
        projected = jnp.dot(centered, basis_full, preferred_element_type=jnp.float32).astype(
            jnp.bfloat16
        )
        image = reduce_image(centered, projected) / total_rows
        local_gram = jnp.dot(image.T, image, precision=lax.Precision.HIGHEST)
        gram = lax.psum(local_gram, ("cluster", "member"))
        lower = jnp.linalg.cholesky(gram)
        orthonormal = jax.scipy.linalg.solve_triangular(lower, image.T, lower=True).T
        basis_full = spread_basis(orthonormal.astype(jnp.bfloat16))
    subspace = orthonormal * math.sqrt(D)
    coords = jnp.dot(centered, basis_full, preferred_element_type=jnp.float32)
    unit = (coords * lax.rsqrt(jnp.sum(coords * coords, axis=1, keepdims=True) + EPS)).astype(
        jnp.bfloat16
    )
    label_values = cluster_ids.astype(jnp.bfloat16)
    limit = valid_counts[0]
    own_index = lax.axis_index("member") * row_count + jnp.arange(row_count, dtype=jnp.int32)
    initial = jnp.full((row_count,), -1.0, jnp.float32)
    piece_units = lax.all_gather(unit, "member", axis=0, tiled=True)
    piece_labels = lax.all_gather(label_values, "member", axis=0, tiled=True)
    scores = lax.dot_general(
        unit, piece_units, (((1,), (1,)), ((), ())), preferred_element_type=jnp.float32
    )
    others = jnp.arange(piece_units.shape[0], dtype=jnp.int32)
    allowed = (
        (label_values[:, None] == piece_labels[None, :])
        & (others[None, :] < limit)
        & (others[None, :] != own_index[:, None])
    )
    nearest = jnp.maximum(initial, jnp.max(jnp.where(allowed, scores, -1.0), axis=1))
    return (subspace, nearest)


def solution(mesh):
    placed = (
        P(("cluster", "member"), None),
        P(("cluster", "member"), None),
        P(("cluster", "member")),
        P("cluster"),
    )
    return jax.shard_map(
        body,
        mesh=mesh,
        in_specs=placed,
        out_specs=(P(("cluster", "member"), None), P(("cluster", "member"))),
        check_vma=False,
    )
```

profile of v0, /device:TPU:0, one launch (start us, length us, event | category | flops | bytes accessed | tf_op | source)
XLA Modules:
  0.0 1155.7 jit_solution(3383755361846079378)
XLA Ops:
  9.9 42.8 %psum.21 = f32[4096]{0:T(1024)S(1)} all-reduce(f32[4096]{0:T(1024)S(1)} %bitcast.117), channel_id=1, replica_groups=mesh['cluster'=4,'member'=8] {'cluster','member'}, use_global_device_ids=true, to_apply=%region_0.0 | all-reduce | flops 4096 | bytes 32768 | tf_op jit(solution)/shard_map/psum | solution.py:32
  52.8 22.7 %all-gather.6.cloned.1.call-done = bf16[4096,512]{1,0:T(8,128)(2,1)} async-done(((bf16[128,512]{1,0:T(8,128)(2,1)}), bf16[4096,512]{1,0:T(8,128)(2,1)}) %all-gather.6.cloned.1.call-update) | async-done | bytes 4194320 | tf_op jit(solution)/shard_map/all_gather | solution.py:13
  83.4 153.1 %reduce-scatter.3.cloned.1.call-done = f32[128,512]{1,0:T(8,128)} async-done(((f32[4096,512]{1,0:T(8,128)}), f32[128,512]{1,0:T(8,128)}) %reduce-scatter.3.cloned.1.call-update) | async-done | bytes 262160 | tf_op jit(solution)/shard_map/reduce_scatter | solution.py:17
  240.5 129.6 %all-reduce.4.cloned.1.call-done = f32[512,512]{0,1:T(8,128)} async-done(((f32[512,512]{0,1:T(8,128)}), f32[512,512]{0,1:T(8,128)}) %all-reduce.4.cloned.1.call-update) | async-done | bytes 1048592 | tf_op jit(solution)/shard_map/psum | solution.py:42
  375.3 11.7 %cholesky.286 = f32[128,128]{1,0:T(8,128)S(1)} custom-call(f32[128,128]{1,0:T(8,128)S(1)} %cholesky.426), custom_call_target="Cholesky" | custom-call | tf_op jit(solution)/shard_map/jit(cholesky)/cholesky | solution.py:43
  400.7 11.7 %cholesky.305 = f32[128,128]{1,0:T(8,128)S(1)} custom-call(f32[128,128]{1,0:T(8,128)S(1)} %cholesky.430), custom_call_target="Cholesky" | custom-call | tf_op jit(solution)/shard_map/jit(cholesky)/cholesky | solution.py:43
  412.9 10.3 custom-call.28
  426.3 13.2 %cholesky.326 = f32[128,128]{1,0:T(8,128)} custom-call(f32[128,128]{1,0:T(8,128)} %cholesky.435), custom_call_target="Cholesky" | custom-call | tf_op jit(solution)/shard_map/jit(cholesky)/cholesky | solution.py:43
  441.6 11.3 custom-call.29
  455.1 11.7 %cholesky.343 = f32[128,128]{1,0:T(8,128)S(1)} custom-call(f32[128,128]{1,0:T(8,128)S(1)} %convolution_subtract_fusion.11), custom_call_target="Cholesky" | custom-call | tf_op jit(solution)/shard_map/jit(cholesky)/cholesky | solution.py:43
  472.6 12.0 %while.4 = (s32[]{:T(128)}, f32[512,512]{1,0:T(8,128)}, s32[4,2]{0,1:T(2,128)S(1)}, f32[4,128,128]{2,1,0:T(8,128)S(1)}, s32[]{:T(128)}) while((s32[]{:T(128)}, f32[512,512]{1,0:T(8,128)}, s32[4,2]{0,1:T(2,128)S(1)}, f32[4,128,128]{2,1,0:T(8,128)S(1)}, s32[]{:T(128)}) %tuple.59), condition=%wide.while_cond, body=%wide.while_body.sunk | while | flops 2 | bytes 131181 | solution.py:44
  485.2 39.3 %custom-call.30 = f32[4,128,128]{1,2,0:T(8,128)S(1)} custom-call(f32[4,128,128]{2,1,0:T(8,128)S(1)} %get-tuple-element.18), custom_call_target="InvertDiagBlocksLowerTriangular" | custom-call | tf_op jit(solution)/shard_map/jit(_solve_triangular)/triangular_solve | solution.py:44
  530.3 64.1 %all-gather.8.cloned.1.call-done = bf16[4096,512]{0,1:T(8,128)(2,1)} async-done(((bf16[128,512]{0,1:T(8,128)(2,1)}), bf16[4096,512]{0,1:T(8,128)(2,1)}) %all-gather.8.cloned.1.call-update) | async-done | bytes 4194320 | tf_op jit(solution)/shard_map/all_gather | solution.py:13
  602.5 152.4 %reduce-scatter.5.cloned.1.call-done = f32[128,512]{1,0:T(8,128)} async-done(((f32[4096,512]{1,0:T(8,128)}), f32[128,512]{1,0:T(8,128)}) %reduce-scatter.5.cloned.1.call-update) | async-done | bytes 262160 | tf_op jit(solution)/shard_map/reduce_scatter | solution.py:17
  758.4 130.1 %all-reduce.6.cloned.1.call-done = f32[512,512]{0,1:T(8,128)} async-done(((f32[512,512]{0,1:T(8,128)}), f32[512,512]{0,1:T(8,128)}) %all-reduce.6.cloned.1.call-update) | async-done | bytes 1048592 | tf_op jit(solution)/shard_map/psum | solution.py:42
  893.6 11.7 %cholesky.358 = f32[128,128]{1,0:T(8,128)S(1)} custom-call(f32[128,128]{1,0:T(8,128)S(1)} %cholesky.439), custom_call_target="Cholesky" | custom-call | tf_op jit(solution)/shard_map/jit(cholesky)/cholesky | solution.py:43
  919.1 11.7 %cholesky.377 = f32[128,128]{1,0:T(8,128)S(1)} custom-call(f32[128,128]{1,0:T(8,128)S(1)} %cholesky.443), custom_call_target="Cholesky" | custom-call | tf_op jit(solution)/shard_map/jit(cholesky)/cholesky | solution.py:43
  946.1 13.2 %cholesky.398 = f32[128,128]{1,0:T(8,128)} custom-call(f32[128,128]{1,0:T(8,128)} %cholesky.448), custom_call_target="Cholesky" | custom-call | tf_op jit(solution)/shard_map/jit(cholesky)/cholesky | solution.py:43
  961.5 11.3 custom-call.33
  975.0 12.3 %cholesky.415 = f32[128,128]{1,0:T(8,128)} custom-call(f32[128,128]{1,0:T(8,128)S(1)} %convolution_subtract_fusion.9), custom_call_target="Cholesky" | custom-call | tf_op jit(solution)/shard_map/jit(cholesky)/cholesky | solution.py:43
  992.7 11.6 %while.5 = (s32[]{:T(128)}, f32[512,512]{1,0:T(8,128)}, s32[4,2]{0,1:T(2,128)S(1)}, f32[4,128,128]{2,1,0:T(8,128)S(1)}, s32[]{:T(128)}) while((s32[]{:T(128)}, f32[512,512]{1,0:T(8,128)}, s32[4,2]{0,1:T(2,128)S(1)}, f32[4,128,128]{2,1,0:T(8,128)S(1)}, s32[]{:T(128)}) %tuple.81), condition=%wide.while_cond.clone, body=%wide.while_body.clone.sunk | while | flops 2 | bytes 131181 | solution.py:44
  1004.3 39.3 %custom-call.34 = f32[4,128,128]{1,2,0:T(8,128)S(1)} custom-call(f32[4,128,128]{2,1,0:T(8,128)S(1)} %get-tuple-element.19), custom_call_target="InvertDiagBlocksLowerTriangular" | custom-call | tf_op jit(solution)/shard_map/jit(_solve_triangular)/triangular_solve | solution.py:44
  1049.4 64.1 %all-gather.10.cloned.1.call-done = bf16[4096,512]{0,1:T(8,128)(2,1)} async-done(((bf16[128,512]{0,1:T(8,128)(2,1)}), bf16[4096,512]{0,1:T(8,128)(2,1)}) %all-gather.10.cloned.1.call-update) | async-done | bytes 4194320 | tf_op jit(solution)/shard_map/all_gather | solution.py:13
  1129.4 16.0 %all-gather.12.cloned.1.call-done = bf16[2048,512]{1,0:T(8,128)(2,1)} async-done(((bf16[256,512]{1,0:T(8,128)(2,1)}), bf16[2048,512]{1,0:T(8,128)(2,1)}) %all-gather.12.cloned.1.call-update) | async-done | bytes 2097168 | tf_op jit(solution)/shard_map/all_gather | solution.py:55
  (152 shorter events, 151.3 us)
Async XLA Ops:
  7.2 68.3 %copy-start = (bf16[256,4096]{1,0:T(8,128)(2,1)S(1)}, bf16[256,4096]{1,0:T(8,128)(2,1)}, u32[]{:S(2)}) copy-start(bf16[256,4096]{1,0:T(8,128)(2,1)} %param.7) | copy-start | bytes 6291460
  7.2 68.3 %all-gather.6.cloned.1.call-start = ((), (), s32[]{:S(2)}) async-start(), calls=%async_computation.2 | async-start | bytes 4325376 | tf_op jit(solution)/shard_map/all_gather | solution.py:13
  7.9 228.5 %reduce-scatter.3.cloned.1.call-start = ((), (), s32[]{:S(2)}) async-start(), calls=%async_computation.3 | async-start | bytes 8650752 | tf_op jit(solution)/shard_map/reduce_scatter | solution.py:17
  83.3 286.8 %all-reduce.4.cloned.1.call-start = ((), (), s32[]{:S(2)}) async-start(), calls=%async_computation.4 | async-start | bytes 2097152 | tf_op jit(solution)/shard_map/psum | solution.py:42
  236.4 4.1 copy-start.5
  239.6 354.8 %all-gather.8.cloned.1.call-start = ((), (), s32[]{:S(2)}) async-start(), calls=%async_computation.5 | async-start | bytes 4325376 | tf_op jit(solution)/shard_map/all_gather | solution.py:13
  370.1 2.7 copy-start.1
  374.3 1.0 copy-start.4
  400.0 0.7 copy-start.8
  466.8 5.8 copy-start.12
  484.7 0.6 copy-start.9
  530.3 224.6 %reduce-scatter.5.cloned.1.call-start = ((), (), s32[]{:S(2)}) async-start(), calls=%async_computation.6 | async-start | bytes 8650752 | tf_op jit(solution)/shard_map/reduce_scatter | solution.py:17
  602.4 286.0 %all-reduce.6.cloned.1.call-start = ((), (), s32[]{:S(2)}) async-start(), calls=%async_computation.7 | async-start | bytes 2097152 | tf_op jit(solution)/shard_map/psum | solution.py:42
  754.9 3.5 copy-start.6
  758.1 355.5 %all-gather.10.cloned.1.call-start = ((), (), s32[]{:S(2)}) async-start(), calls=%async_computation.8 | async-start | bytes 4325376 | tf_op jit(solution)/shard_map/all_gather | solution.py:13
  888.5 2.7 copy-start.2
  892.6 1.0 copy-start.3
  918.4 0.7 copy-start.7
  973.8 18.9 %copy-start.10 = (s32[4,2]{0,1:T(2,128)S(1)}, s32[4,2]{0,1:T(2,128)}, u32[]{:S(2)}) copy-start(s32[4,2]{0,1:T(2,128)} %copy-done.9) | copy-start | bytes 100
  1049.3 68.6 %copy-start.11 = (s32[256]{0:T(256)S(1)}, s32[256]{0:T(256)}, u32[]{:S(2)}) copy-start(s32[256]{0:T(256)} %param.9) | copy-start | bytes 3076
  1049.3 96.1 %all-gather.12.cloned.1.call-start = ((), (), s32[]{:S(2)}) async-start(), calls=%async_computation.9 | async-start | bytes 2359296 | tf_op jit(solution)/shard_map/all_gather | solution.py:55
Sparse Core Ops, SparseCore 0:
  11.0 64.3 all-gather.5
  83.5 152.9 reduce-scatter.2
  241.6 128.4 all-reduce.3
  530.4 64.0 all-gather.7
  602.5 152.2 reduce-scatter.4
  759.9 128.4 all-reduce.5
  1049.4 64.0 all-gather.9
  1118.1 27.3 all-gather.11
where the time goes:
time: 1160 us
  waiting for transfers between devices  733 us (63%)
  other arithmetic  259 us (22%)
  matrix products  54.7 us (5%)
  blocking collectives  52.6 us (5%)
  local copies, waits for them, and re-layouts  35.1 us (3%)
  between operations  20.6 us (2%)
    reduce_scatter x2, waiting for transfers between devices, reduce_image(): lax.psum_scatter(lax.dot_general(centered, projected, (((0,), (0,)), ((),...  305 us
    psum x2, waiting for transfers between devices, body(): gram = lax.psum(local_gram, ('cluster', 'member'))  260 us
    another operation x29, other arithmetic, body(): lower = jnp.linalg.cholesky(gram)  172 us
    all_gather x3, waiting for transfers between devices, spread_basis(): return lax.all_gather(local_rows, ('cluster', 'member'), axis=0, tiled=True)  151 us
    another operation x5, other arithmetic, body(): jax.scipy.linalg.solve_triangular(lower, image.T, lower=True)  81.4 us
    psum x1, blocking collectives, body(): average = lax.psum(column_sums, ('cluster', 'member')) / total_rows  42.8 us
    another operation x27, local copies, waits for them, and re-layouts, body(): jax.scipy.linalg.solve_triangular(lower, image.T, lower=True)  23.5 us
  transfers between devices with their start and end apart: 8, of which 8 were waited for; matrix products, arithmetic and copies ran while one was open for 0% of the time, Pallas kernels for 0%

commit v1 on v0

--- a/solution.py
+++ b/solution.py
@@ -39,7 +39,7 @@
         )
         image = reduce_image(centered, projected) / total_rows
         local_gram = jnp.dot(image.T, image, precision=lax.Precision.HIGHEST)
-        gram = lax.psum(local_gram, ("cluster", "member"))
+        gram = lax.psum(lax.psum(local_gram, "member"), "cluster")
         lower = jnp.linalg.cholesky(gram)
         orthonormal = jax.scipy.linalg.solve_triangular(lower, image.T, lower=True).T
         basis_full = spread_basis(orthonormal.astype(jnp.bfloat16))

time: 1160 us -> 1130 us (0.974)
  waiting for transfers between devices: 733 us -> 697 us
    psum x2 -> x4, waiting for transfers between devices: 260 us -> 222 us  [body(): gram = lax.psum(lax.psum(local_gram, 'member'), 'cluster')]
  transfers between devices with their start and end apart: 8 -> 10, of which waited for: 8 -> 10; matrix products, arithmetic and copies ran while one was open for 0% -> 0% of each run, Pallas kernels for 0% -> 0%
where the time goes in v1:
time: 1130 us; the launch traced here: 1120 us
  waiting for transfers between devices  697 us (62%)
  other arithmetic  259 us (23%)
  matrix products  54.7 us (5%)
  blocking collectives  52.7 us (5%)
  local copies, waits for them, and re-layouts  35 us (3%)
  between operations  20.6 us (2%)
    reduce_scatter x2, waiting for transfers between devices, reduce_image(): lax.psum_scatter(lax.dot_general(centered, projected, (((0,), (0,)), ((),...  305 us
    psum x4, waiting for transfers between devices, body(): gram = lax.psum(lax.psum(local_gram, 'member'), 'cluster')  222 us
    another operation x29, other arithmetic, body(): lower = jnp.linalg.cholesky(gram)  172 us
    all_gather x3, waiting for transfers between devices, spread_basis(): return lax.all_gather(local_rows, ('cluster', 'member'), axis=0, tiled=True)  153 us
    another operation x5, other arithmetic, body(): jax.scipy.linalg.solve_triangular(lower, image.T, lower=True)  81.4 us
    psum x1, blocking collectives, body(): average = lax.psum(column_sums, ('cluster', 'member')) / total_rows  42.8 us
    another operation x27, local copies, waits for them, and re-layouts, body(): jax.scipy.linalg.solve_triangular(lower, image.T, lower=True)  23.5 us
  transfers between devices with their start and end apart: 10, of which 10 were waited for; matrix products, arithmetic and copies ran while one was open for 0% of the time, Pallas kernels for 0%

profile of v1, /device:TPU:0, one launch (start us, length us, event | category | flops | bytes accessed | tf_op | source)
XLA Modules:
  0.0 1120.2 jit_solution(9118268415937341258)
XLA Ops:
  9.9 42.8 %psum.35 = f32[4096]{0:T(1024)S(1)} all-reduce(f32[4096]{0:T(1024)S(1)} %bitcast.117), channel_id=1, replica_groups=mesh['cluster'=4,'member'=8] {'cluster','member'}, use_global_device_ids=true, to_apply=%region_0.0 | all-reduce | flops 4096 | bytes 32768 | tf_op jit(solution)/shard_map/psum | solution.py:32
  52.8 22.7 %all-gather.6.cloned.1.call-done = bf16[4096,512]{1,0:T(8,128)(2,1)} async-done(((bf16[128,512]{1,0:T(8,128)(2,1)}), bf16[4096,512]{1,0:T(8,128)(2,1)}) %all-gather.6.cloned.1.call-update) | async-done | bytes 4194320 | tf_op jit(solution)/shard_map/all_gather | solution.py:13
  83.4 152.6 %reduce-scatter.3.cloned.1.call-done = f32[128,512]{1,0:T(8,128)} async-done(((f32[4096,512]{1,0:T(8,128)}), f32[128,512]{1,0:T(8,128)}) %reduce-scatter.3.cloned.1.call-update) | async-done | bytes 262160 | tf_op jit(solution)/shard_map/reduce_scatter | solution.py:17
  239.3 57.3 %all-reduce.6.cloned.1.call-done = f32[512,512]{0,1:T(8,128)} async-done(((f32[512,512]{0,1:T(8,128)}), f32[512,512]{0,1:T(8,128)}) %all-reduce.6.cloned.1.call-update) | async-done | bytes 1048592 | tf_op jit(solution)/shard_map/psum | solution.py:42
  297.5 53.6 %all-reduce.8.cloned.1.call-done = f32[512,512]{0,1:T(8,128)} async-done(((f32[512,512]{0,1:T(8,128)}), f32[512,512]{0,1:T(8,128)}) %all-reduce.8.cloned.1.call-update) | async-done | bytes 1048592 | tf_op jit(solution)/shard_map/psum | solution.py:42
  356.2 11.7 %cholesky.286 = f32[128,128]{1,0:T(8,128)S(1)} custom-call(f32[128,128]{1,0:T(8,128)S(1)} %cholesky.426), custom_call_target="Cholesky" | custom-call | tf_op jit(solution)/shard_map/jit(cholesky)/cholesky | solution.py:43
  381.6 11.7 %cholesky.305 = f32[128,128]{1,0:T(8,128)S(1)} custom-call(f32[128,128]{1,0:T(8,128)S(1)} %cholesky.430), custom_call_target="Cholesky" | custom-call | tf_op jit(solution)/shard_map/jit(cholesky)/cholesky | solution.py:43
  407.2 13.2 %cholesky.326 = f32[128,128]{1,0:T(8,128)} custom-call(f32[128,128]{1,0:T(8,128)} %cholesky.435), custom_call_target="Cholesky" | custom-call | tf_op jit(solution)/shard_map/jit(cholesky)/cholesky | solution.py:43
  422.5 11.3 %custom-call.29 = f32[1,128,128]{1,2,0:T(8,128)} custom-call(f32[1,128,128]{2,1,0:T(8,128)} %get-tuple-element.59), custom_call_target="InvertDiagBlocksLowerTriangular" | custom-call | tf_op jit(solution)/shard_map/jit(cholesky)/cholesky | solution.py:43
  436.0 11.7 %cholesky.343 = f32[128,128]{1,0:T(8,128)S(1)} custom-call(f32[128,128]{1,0:T(8,128)S(1)} %convolution_subtract_fusion.11), custom_call_target="Cholesky" | custom-call | tf_op jit(solution)/shard_map/jit(cholesky)/cholesky | solution.py:43
  453.5 12.0 %while.4 = (s32[]{:T(128)}, f32[512,512]{1,0:T(8,128)}, s32[4,2]{0,1:T(2,128)S(1)}, f32[4,128,128]{2,1,0:T(8,128)S(1)}, s32[]{:T(128)}) while((s32[]{:T(128)}, f32[512,512]{1,0:T(8,128)}, s32[4,2]{0,1:T(2,128)S(1)}, f32[4,128,128]{2,1,0:T(8,128)S(1)}, s32[]{:T(128)}) %tuple.59), condition=%wide.while_cond, body=%wide.while_body.sunk | while | flops 2 | bytes 131181 | solution.py:44
  466.1 39.3 %custom-call.30 = f32[4,128,128]{1,2,0:T(8,128)S(1)} custom-call(f32[4,128,128]{2,1,0:T(8,128)S(1)} %get-tuple-element.18), custom_call_target="InvertDiagBlocksLowerTriangular" | custom-call | tf_op jit(solution)/shard_map/jit(_solve_triangular)/triangular_solve | solution.py:44
  511.2 65.2 %all-gather.8.cloned.1.call-done = bf16[4096,512]{0,1:T(8,128)(2,1)} async-done(((bf16[128,512]{0,1:T(8,128)(2,1)}), bf16[4096,512]{0,1:T(8,128)(2,1)}) %all-gather.8.cloned.1.call-update) | async-done | bytes 4194320 | tf_op jit(solution)/shard_map/all_gather | solution.py:13
  584.4 152.6 %reduce-scatter.5.cloned.1.call-done = f32[128,512]{1,0:T(8,128)} async-done(((f32[4096,512]{1,0:T(8,128)}), f32[128,512]{1,0:T(8,128)}) %reduce-scatter.5.cloned.1.call-update) | async-done | bytes 262160 | tf_op jit(solution)/shard_map/reduce_scatter | solution.py:17
  740.2 57.1 %all-reduce.10.cloned.1.call-done = f32[512,512]{0,1:T(8,128)} async-done(((f32[512,512]{0,1:T(8,128)}), f32[512,512]{0,1:T(8,128)}) %all-reduce.10.cloned.1.call-update) | async-done | bytes 1048592 | tf_op jit(solution)/shard_map/psum | solution.py:42
  797.6 54.3 %all-reduce.12.cloned.1.call-done = f32[512,512]{0,1:T(8,128)} async-done(((f32[512,512]{0,1:T(8,128)}), f32[512,512]{0,1:T(8,128)}) %all-reduce.12.cloned.1.call-update) | async-done | bytes 1048592 | tf_op jit(solution)/shard_map/psum | solution.py:42
  857.0 11.7 %cholesky.358 = f32[128,128]{1,0:T(8,128)S(1)} custom-call(f32[128,128]{1,0:T(8,128)S(1)} %cholesky.439), custom_call_target="Cholesky" | custom-call | tf_op jit(solution)/shard_map/jit(cholesky)/cholesky | solution.py:43
  882.5 11.7 %cholesky.377 = f32[128,128]{1,0:T(8,128)S(1)} custom-call(f32[128,128]{1,0:T(8,128)S(1)} %cholesky.443), custom_call_target="Cholesky" | custom-call | tf_op jit(solution)/shard_map/jit(cholesky)/cholesky | solution.py:43
  909.5 13.2 %cholesky.398 = f32[128,128]{1,0:T(8,128)} custom-call(f32[128,128]{1,0:T(8,128)} %cholesky.448), custom_call_target="Cholesky" | custom-call | tf_op jit(solution)/shard_map/jit(cholesky)/cholesky | solution.py:43
  938.5 12.3 %cholesky.415 = f32[128,128]{1,0:T(8,128)} custom-call(f32[128,128]{1,0:T(8,128)S(1)} %convolution_subtract_fusion.9), custom_call_target="Cholesky" | custom-call | tf_op jit(solution)/shard_map/jit(cholesky)/cholesky | solution.py:43
  956.1 11.6 %while.5 = (s32[]{:T(128)}, f32[512,512]{1,0:T(8,128)}, s32[4,2]{0,1:T(2,128)S(1)}, f32[4,128,128]{2,1,0:T(8,128)S(1)}, s32[]{:T(128)}) while((s32[]{:T(128)}, f32[512,512]{1,0:T(8,128)}, s32[4,2]{0,1:T(2,128)S(1)}, f32[4,128,128]{2,1,0:T(8,128)S(1)}, s32[]{:T(128)}) %tuple.85), condition=%wide.while_cond.clone, body=%wide.while_body.clone.sunk | while | flops 2 | bytes 131181 | solution.py:44
  967.7 39.3 %custom-call.34 = f32[4,128,128]{1,2,0:T(8,128)S(1)} custom-call(f32[4,128,128]{2,1,0:T(8,128)S(1)} %get-tuple-element.19), custom_call_target="InvertDiagBlocksLowerTriangular" | custom-call | tf_op jit(solution)/shard_map/jit(_solve_triangular)/triangular_solve | solution.py:44
  1012.8 65.2 %all-gather.10.cloned.1.call-done = bf16[4096,512]{0,1:T(8,128)(2,1)} async-done(((bf16[128,512]{0,1:T(8,128)(2,1)}), bf16[4096,512]{0,1:T(8,128)(2,1)}) %all-gather.10.cloned.1.call-update) | async-done | bytes 4194320 | tf_op jit(solution)/shard_map/all_gather | solution.py:13
  1093.9 16.0 %all-gather.12.cloned.1.call-done = bf16[2048,512]{1,0:T(8,128)(2,1)} async-done(((bf16[256,512]{1,0:T(8,128)(2,1)}), bf16[2048,512]{1,0:T(8,128)(2,1)}) %all-gather.12.cloned.1.call-update) | async-done | bytes 2097168 | tf_op jit(solution)/shard_map/all_gather | solution.py:55
  (158 shorter events, 172.9 us)
Async XLA Ops:
  7.2 68.3 %copy-start = (bf16[256,4096]{1,0:T(8,128)(2,1)S(1)}, bf16[256,4096]{1,0:T(8,128)(2,1)}, u32[]{:S(2)}) copy-start(bf16[256,4096]{1,0:T(8,128)(2,1)} %param.7) | copy-start | bytes 6291460
  7.2 68.3 %all-gather.6.cloned.1.call-start = ((), (), s32[]{:S(2)}) async-start(), calls=%async_computation.2 | async-start | bytes 4325376 | tf_op jit(solution)/shard_map/all_gather | solution.py:13
  7.9 228.1 %reduce-scatter.3.cloned.1.call-start = ((), (), s32[]{:S(2)}) async-start(), calls=%async_computation.3 | async-start | bytes 8650752 | tf_op jit(solution)/shard_map/reduce_scatter | solution.py:17
  83.3 213.2 %all-reduce.6.cloned.1.call-start = ((), (), s32[]{:S(2)}) async-start(), calls=%async_computation.4 | async-start | bytes 2097152 | tf_op jit(solution)/shard_map/psum | solution.py:42
  236.0 61.4 %copy-start.5 = (f32[128,512]{1,0:T(8,128)S(1)}, f32[128,512]{1,0:T(8,128)}, u32[]{:S(2)}) copy-start(f32[128,512]{1,0:T(8,128)} %reduce-scatter.3.cloned.1.call-done) | copy-start | bytes 786436
  239.2 111.8 %all-reduce.8.cloned.1.call-start = ((), (), s32[]{:S(2)}) async-start(), calls=%async_computation.5 | async-start | bytes 2097152 | tf_op jit(solution)/shard_map/psum | solution.py:42
  296.6 279.8 %all-gather.8.cloned.1.call-start = ((), (), s32[]{:S(2)}) async-start(), calls=%async_computation.6 | async-start | bytes 4325376 | tf_op jit(solution)/shard_map/all_gather | solution.py:13
  351.1 2.6 copy-start.1
  355.2 1.0 copy-start.4
  380.9 0.7 copy-start.8
  447.7 5.8 copy-start.12
  465.6 0.6 copy-start.9
  511.2 225.8 %reduce-scatter.5.cloned.1.call-start = ((), (), s32[]{:S(2)}) async-start(), calls=%async_computation.7 | async-start | bytes 8650752 | tf_op jit(solution)/shard_map/reduce_scatter | solution.py:17
  584.4 212.9 %all-reduce.10.cloned.1.call-start = ((), (), s32[]{:S(2)}) async-start(), calls=%async_computation.8 | async-start | bytes 2097152 | tf_op jit(solution)/shard_map/psum | solution.py:42
  737.0 60.6 %copy-start.6 = (f32[128,512]{1,0:T(8,128)S(1)}, f32[128,512]{1,0:T(8,128)}, u32[]{:S(2)}) copy-start(f32[128,512]{1,0:T(8,128)} %reduce-scatter.5.cloned.1.call-done) | copy-start | bytes 786436
  740.2 111.7 %all-reduce.12.cloned.1.call-start = ((), (), s32[]{:S(2)}) async-start(), calls=%async_computation.9 | async-start | bytes 2097152 | tf_op jit(solution)/shard_map/psum | solution.py:42
  797.3 280.7 %all-gather.10.cloned.1.call-start = ((), (), s32[]{:S(2)}) async-start(), calls=%async_computation.10 | async-start | bytes 4325376 | tf_op jit(solution)/shard_map/all_gather | solution.py:13
  851.9 2.6 copy-start.2
  856.0 1.0 copy-start.3
  881.8 0.7 copy-start.7
  937.2 18.9 %copy-start.10 = (s32[4,2]{0,1:T(2,128)S(1)}, s32[4,2]{0,1:T(2,128)}, u32[]{:S(2)}) copy-start(s32[4,2]{0,1:T(2,128)} %copy-done.9) | copy-start | bytes 100
  1012.8 69.7 %copy-start.11 = (s32[256]{0:T(256)S(1)}, s32[256]{0:T(256)}, u32[]{:S(2)}) copy-start(s32[256]{0:T(256)} %param.9) | copy-start | bytes 3076
  1012.8 97.1 %all-gather.12.cloned.1.call-start = ((), (), s32[]{:S(2)}) async-start(), calls=%async_computation.11 | async-start | bytes 2359296 | tf_op jit(solution)/shard_map/all_gather | solution.py:55
Sparse Core Ops, SparseCore 0:
  11.0 64.3 all-gather.5
  83.5 152.5 reduce-scatter.2
  239.3 57.1 all-reduce.5
  299.5 51.5 all-reduce.7
  511.3 65.0 all-gather.7
  584.5 152.4 reduce-scatter.4
  740.3 56.9 all-reduce.9
  800.4 51.5 all-reduce.11
  1012.9 65.0 all-gather.9
  1082.6 27.3 all-gather.11
